TPU v7x, 128 devices: a whole 4x4x4 slice. The times are simulated.
128 devices in a mesh: rows: 4 (over z_hi, core), cols: 32 (over x, z_lo, y).
Axes of the slice: x: 4, y: 4, z: 4 (z_hi: 2, z_lo: 2; z = z_hi * 2 + z_lo), core: 2. Of those that a mesh axis runs over, the one named last changes fastest.
Arguments:
- tokens: bfloat16 [2048, 6144], P('rows', 'cols'), may hold values from -6 to 6
- cotangent: bfloat16 [2048, 16384], P('rows', 'cols'), may hold values from -0.049804688 to 0.049804688
- weight: bfloat16 [6144, 16384], P(None, 'cols'), may hold values from -6 to 6
- momentum: float32 [128, 768, 1024], P(('rows', 'cols')), may hold values from -40 to 40
Outputs:
- new_weight: bfloat16 [6144, 16384], P(None, 'cols')
- input_grad: bfloat16 [2048, 6144], P('rows', 'cols')
- new_momentum: float32 [128, 768, 1024], P(('rows', 'cols'))
- update: float32 [128, 768, 1024], P(('rows', 'cols'))
All inputs are finite; a program needn't handle non-finite values.
Results may differ from a plain program's by a relative error of at most 0.012.
Values may be sent and summed in bfloat16 or wider, within the bound.
A program may use at most 128 MiB of HBM per device.

v0:
```python
import jax
import jax.numpy as jnp
from jax import lax
from jax.sharding import Mesh
from jax.sharding import PartitionSpec as P

NS_STEPS = 2
COLS = ("cols_0", "cols_1", "cols_2")
ROWS_COLS = ("rows", "cols_0", "cols_1", "cols_2")
coef_a = 3.4445
coef_b = -4.775
coef_c = 2.0315
beta_mom = 0.95
step_rate = 0.25


def reduced_to_own(pieces, axes, sequence):
    inside = pieces.shape[1:]
    pieces = pieces.reshape(*(lax.axis_size(a) for a in axes), *inside)
    pieces = jnp.moveaxis(pieces, sequence, range(len(axes))).reshape(-1, *inside)
    for k in sequence:
        pieces = lax.psum_scatter(pieces, axes[k], scatter_dimension=0, tiled=True)
    return pieces[0]


def cut_along(x, dim, count):
    before, after = (x.shape[:dim], x.shape[dim + 1 :])
    return jnp.moveaxis(x.reshape(*before, count, -1, *after), dim, 0)


def summed_rows(x, axes, sequence, dim):
    count = lax.axis_size(axes)
    return reduced_to_own(cut_along(x, dim, count), axes, sequence)


def partner(x, axis, bit):
    return lax.ppermute(x, axis, [(i, i ^ 1 << bit) for i in range(lax.axis_size(axis))])


def orthogonalize(matrix):
    norm_value = jnp.sqrt(jnp.sum(matrix * matrix))
    current = (matrix / (norm_value + 1e-07)).astype(jnp.bfloat16)
    for index in range(NS_STEPS):
        square = jnp.dot(current, current.T, preferred_element_type=jnp.float32).astype(
            jnp.bfloat16
        )
        poly = (
            coef_b * square.astype(jnp.float32)
            + coef_c * jnp.dot(square, square, preferred_element_type=jnp.float32)
        ).astype(jnp.bfloat16)
        current = (
            coef_a * current.astype(jnp.float32)
            + jnp.dot(poly, current, preferred_element_type=jnp.float32)
        ).astype(jnp.bfloat16)
    return current


def body(tokens, cotangent, weight, momentum):
    half_bit = lax.axis_index(COLS) % 2
    other_bit = 1 - half_bit
    groups = lax.axis_size("rows")
    partial_value = lax.dot_general(
        lax.all_gather(tokens, COLS, axis=1, tiled=True),
        cotangent,
        (((0,), (0,)), ((), ())),
        preferred_element_type=jnp.float32,
    )
    terms = lax.dot_general(
        cotangent, weight, (((1,), (1,)), ((), ())), preferred_element_type=jnp.float32
    )
    input_grad = summed_rows(terms, COLS, (0, 2, 1), 1).astype(jnp.bfloat16)
    d_rows, f_cols = partial_value.shape
    block_rows = d_rows // (2 * groups)
    summed = lax.psum_scatter(partial_value, "rows", scatter_dimension=0, tiled=True)
    split = summed.reshape(2, block_rows, f_cols)
    mine = lax.dynamic_index_in_dim(split, half_bit, 0, keepdims=False)
    theirs = lax.dynamic_index_in_dim(split, other_bit, 0, keepdims=False)
    received = partner(theirs, COLS, 0)
    joined = jnp.where(
        half_bit == 0, jnp.concatenate([mine, received], 1), jnp.concatenate([received, mine], 1)
    )
    grad_block = joined[None]
    new_momentum = beta_mom * momentum + grad_block
    block_cols = new_momentum.shape[2]
    scale_value = float(max(block_rows, block_cols)) ** 0.5
    update = scale_value * orthogonalize(new_momentum[0]).astype(jnp.float32)
    sent = update.astype(jnp.bfloat16)
    col_split = sent.reshape(block_rows, 2, f_cols)
    mine = lax.dynamic_index_in_dim(col_split, half_bit, 1, keepdims=False)
    theirs = lax.dynamic_index_in_dim(col_split, other_bit, 1, keepdims=False)
    received = partner(theirs, COLS, 0)
    stacked = jnp.where(
        half_bit == 0, jnp.concatenate([mine, received], 0), jnp.concatenate([received, mine], 0)
    )
    placed = lax.all_gather(stacked, "rows", axis=0, tiled=True)
    new_weight = (weight.astype(jnp.float32) - step_rate * placed.astype(jnp.float32)).astype(
        jnp.bfloat16
    )
    return (new_weight, input_grad, new_momentum, update[None])


def solution(mesh):
    torus = Mesh(
        mesh.devices.reshape(mesh.shape["rows"], 4, 2, 4), ("rows", "cols_0", "cols_1", "cols_2")
    )
    in_specs = (P("rows", COLS), P("rows", COLS), P(None, COLS), P(ROWS_COLS, None, None))
    out_specs = (P(None, COLS), P("rows", COLS), P(ROWS_COLS, None, None), P(ROWS_COLS, None, None))
    return jax.shard_map(body, mesh=torus, in_specs=in_specs, out_specs=out_specs, check_vma=False)
```

profile of v0, /device:TPU:1, one launch (start us, length us, event | category | flops | bytes accessed | tf_op | source)
XLA Modules:
  0.0 557.8 jit_solution(7268899705757204786)
XLA Ops:
  8.1 0.7 all-gather.3.cloned.1.call-update
  8.8 0.2 copy-done
  9.0 9.2 %fusion.15 = f32[512,6144]{0,1:T(8,128)} fusion(bf16[512,512]{1,0:T(8,128)(2,1)S(1)} %copy-done, bf16[6144,512]{1,0:T(8,128)(2,1)} %param.6), kind=kOutput, calls=%fused_computation.30 | convolution fusion | flops 3221225472 | bytes 19398656 | tf_op jit(solution)/shard_map/dot_general | solution.py:68
  18.3 11.6 %copy.15 = f32[4,4,2,512,192]{3,4,2,1,0:T(8,128)} copy(f32[4,4,2,512,192]{3,4,1,2,0:T(8,128)} %bitcast.40) | data formatting | bytes 25165824 | tf_op jit(solution)/shard_map/transpose | solution.py:20
  29.9 214.0 %all-gather.3.cloned.1.call-done = bf16[512,6144]{0,1:T(8,128)(2,1)} async-done(((bf16[512,192]{0,1:T(8,128)(2,1)}), bf16[512,6144]{0,1:T(8,128)(2,1)}) %all-gather.3.cloned.1.call-update) | async-done | bytes 6291472 | tf_op jit(solution)/shard_map/all_gather | solution.py:63
  244.0 9.2 %fusion.14 = f32[6144,512]{1,0:T(8,128)} fusion(bf16[512,6144]{0,1:T(8,128)(2,1)} %all-gather.3.cloned.1.call-done, bf16[512,512]{1,0:T(8,128)(2,1)S(1)} %copy-done), kind=kOutput, calls=%fused_computation.29 | convolution fusion | flops 3221225472 | bytes 19398656 | tf_op jit(solution)/shard_map/dot_general | solution.py:62
  253.3 0.5 reduce-scatter.9.cloned.1.call-update
  253.8 121.0 %reduce-scatter.5.cloned.1.call-done = f32[1536,512]{1,0:T(8,128)} async-done(((f32[6144,512]{1,0:T(8,128)}), f32[1536,512]{1,0:T(8,128)}) %reduce-scatter.5.cloned.1.call-update) | async-done | bytes 3145744 | tf_op jit(solution)/shard_map/reduce_scatter | solution.py:74
  374.9 3.3 dynamic-slice_bitcast_fusion
  378.2 1.2 collective-permute-start
  379.4 59.6 %reduce-scatter.9.cloned.1.call-done = f32[2,512,192]{1,2,0:T(8,128)} async-done(((f32[8,512,192]{1,2,0:T(8,128)}), f32[2,512,192]{1,2,0:T(8,128)}) %reduce-scatter.9.cloned.1.call-update) | async-done | bytes 786448 | tf_op jit(solution)/shard_map/reduce_scatter | solution.py:22
  439.3 6.2 %multiply_reduce_fusion = (f32[]{:T(128)}, f32[1,768,1024]{2,1,0:T(8,128)}) fusion(f32[1,768,512]{2,1,0:T(8,128)S(1)} %get-tuple-element.7, f32[1,768,512]{2,1,0:T(8,128)} %bitcast.2, pred[]{:T(512)S(6)} %eq.6, f32[1,768,1024]{2,1,0:T(8,128)} %param.7), kind=kLoop, calls=%fused_computation.9 | loop fusion | flops 5505023 | bytes 9437189 | tf_op jit(solution)/shard_map/reduce_sum | solution.py:41
  446.2 4.3 fusion.6
  450.5 5.2 add_convert_fusion.1
  455.7 1.4 convolution_convert_fusion
  457.2 4.6 fusion.1
  461.7 2.9 reshape.82
  464.6 3.2 constant_dynamic-slice_fusion.1
  468.1 1.3 collective-permute-start.1
  469.5 16.6 %collective-permute-done.1 = bf16[768,512]{1,0:T(8,128)(2,1)S(1)} collective-permute-done((bf16[768,512]{1,0:T(8,128)(2,1)S(1)}, bf16[768,512]{1,0:T(8,128)(2,1)S(1)}, u32[]{:S(2)}, u32[]{:S(2)}) %collective-permute-start.1) | collective-permute-done | bytes 786464 | tf_op jit(solution)/shard_map/ppermute | solution.py:37
  486.1 1.8 maximum_select_fusion.1
  488.0 1.7 convert_bitcast_fusion
  489.7 51.3 %all-gather.5.cloned.1.call-done = bf16[6144,512]{1,0:T(8,128)(2,1)} async-done(((bf16[1536,512]{1,0:T(8,128)(2,1)}), bf16[6144,512]{1,0:T(8,128)(2,1)}) %all-gather.5.cloned.1.call-update) | async-done | bytes 6291472 | tf_op jit(solution)/shard_map/all_gather | solution.py:95
  541.0 9.2 %subtract_convert_fusion = bf16[6144,512]{1,0:T(8,128)(2,1)} fusion(bf16[6144,512]{1,0:T(8,128)(2,1)} %all-gather.5.cloned.1.call-done, bf16[6144,512]{1,0:T(8,128)(2,1)} %param.6), kind=kLoop, calls=%fused_computation | loop fusion | flops 15728640 | bytes 18874368 | tf_op jit(solution)/shard_map/convert_element_type | solution.py:96
  (18 shorter events, 1.0 us)
Async XLA Ops:
  8.0 1.1 copy-start
  8.0 236.0 %all-gather.3.cloned.1.call-start = ((), (), s32[]{:S(2)}) async-start(), calls=%async_computation.4 | async-start | bytes 6488064 | tf_op jit(solution)/shard_map/all_gather | solution.py:63
  8.7 244.5 %reduce-scatter.7.cloned.1.call-start = ((), (), s32[]{:S(2)}) async-start(), calls=%async_computation.7 | async-start | bytes 15728640 | tf_op jit(solution)/shard_map/reduce_scatter | solution.py:22
  29.9 345.0 %reduce-scatter.5.cloned.1.call-start = ((), (), s32[]{:S(2)}) async-start(), calls=%async_computation.5 | async-start | bytes 15728640 | tf_op jit(solution)/shard_map/reduce_scatter | solution.py:74
  253.2 185.8 %reduce-scatter.9.cloned.1.call-start = ((), (), s32[]{:S(2)}) async-start(), calls=%async_computation.8 | async-start | bytes 3932160 | tf_op jit(solution)/shard_map/reduce_scatter | solution.py:22
  253.8 234.2 %reduce-scatter.11.cloned.1.call-start = ((), (), s32[]{:S(2)}) async-start(), calls=%async_computation.9 | async-start | bytes 1179648 | tf_op jit(solution)/shard_map/reduce_scatter | solution.py:22
  378.2 61.1 %collective-permute-start = (f32[768,512]{1,0:T(8,128)}, f32[768,512]{1,0:T(8,128)}, u32[]{:S(2)}, u32[]{:S(2)}) collective-permute-start(f32[768,512]{1,0:T(8,128)} %get-tuple-element.6), channel_id=1, source_target_pairs={{0,1},{1,0},{2,3},{3,2},{4,5},{5,4},{6,7},{7,6},{8,9},{9,8},{10,11... | collective-permute-start | bytes 4718600 | tf_op jit(solution)/shard_map/ppermute | solution.py:37
  439.1 102.0 %all-gather.5.cloned.1.call-start = ((), (), s32[]{:S(2)}) async-start(), calls=%async_computation.6 | async-start | bytes 7864320 | tf_op jit(solution)/shard_map/all_gather | solution.py:95
  468.1 18.1 %collective-permute-start.1 = (bf16[768,512]{1,0:T(8,128)(2,1)S(1)}, bf16[768,512]{1,0:T(8,128)(2,1)S(1)}, u32[]{:S(2)}, u32[]{:S(2)}) collective-permute-start(bf16[768,512]{1,0:T(8,128)(2,1)S(1)} %bitcast.44), channel_id=1, source_target_pairs={{0,1},{1,0},{2,3},{3,2},{4,5},{5,4},{6,7},{7,6},{8,9},{9,8},{10,11... | collective-permute-start | bytes 2359304 | tf_op jit(solution)/shard_map/ppermute | solution.py:37
  541.0 9.2 %copy-start.1 = (bf16[512,512]{1,0:T(8,128)(2,1)S(1)}, bf16[512,512]{1,0:T(8,128)(2,1)}, u32[]{:S(2)}) copy-start(bf16[512,512]{1,0:T(8,128)(2,1)} %param.5) | copy-start | bytes 1572868
Sparse Core Ops, SparseCore 0:
  10.5 233.4 all-gather.2
Sparse Core Ops, SparseCore 1:
  30.0 128.8 reduce-scatter.6
  253.3 121.6 reduce-scatter.4
  377.2 61.8 reduce-scatter.8
  441.4 20.1 reduce-scatter.10
  488.1 52.9 all-gather.4
where the time goes:
time: 558 us
  waiting for transfers between devices  464 us (83%)
  matrix products  33.9 us (6%)
  local copies, waits for them, and re-layouts  21.7 us (4%)
  other arithmetic  18.9 us (3%)
  between operations  16.5 us (3%)
    all_gather x1, waiting for transfers between devices, body(): lax.all_gather(tokens, COLS, axis=1, tiled=True)  214 us
    reduce_scatter x1, waiting for transfers between devices, body(): lax.psum_scatter(partial_value, 'rows', scatter_dimension=0, tiled=True)  121 us
    reduce_scatter x3, waiting for transfers between devices, reduced_to_own(): pieces = lax.psum_scatter(pieces, axes[k], scatter_dimension=0, tiled=True)  59.7 us
    all_gather x1, waiting for transfers between devices, body(): placed = lax.all_gather(stacked, 'rows', axis=0, tiled=True)  51.3 us
    ppermute x2, waiting for transfers between devices, partner(): lax.ppermute(x, axis, [(i, i ^ 1 << bit) for i in range(lax.axis_size(axi...  16.6 us
    transpose x1, local copies, waits for them, and re-layouts, reduced_to_own(): jnp.moveaxis(pieces, sequence, range(len(axes))).reshape(-1, *inside)  11.6 us
  transfers between devices with their start and end apart: 8, of which 5 were waited for; matrix products, arithmetic and copies ran while one was open for 12% of the time, Pallas kernels for 0%

commit v1 on v0

--- a/solution.py
+++ b/solution.py
@@ -92,7 +92,9 @@
     stacked = jnp.where(
         half_bit == 0, jnp.concatenate([mine, received], 0), jnp.concatenate([received, mine], 0)
     )
-    placed = lax.all_gather(stacked, "rows", axis=0, tiled=True)
+    placed = jnp.concatenate(
+        lax.all_to_all(jnp.stack([stacked] * lax.axis_size("rows")), "rows", 0, 0), axis=0
+    )
     new_weight = (weight.astype(jnp.float32) - step_rate * placed.astype(jnp.float32)).astype(
         jnp.bfloat16
     )

time: 558 us -> 579 us (1.038)
  other arithmetic: 18.9 us -> 29 us
  starting transfers between devices: 2.9 us -> 8.89 us
    reduce_scatter x3, waiting for transfers between devices: 59.7 us -> 144 us  [reduced_to_own(): pieces = lax.psum_scatter(pieces, axes[k], scatter_dimension=0, tiled=True)]
    all_gather x1, waiting for transfers between devices: 214 us -> 146 us  [body(): lax.all_gather(tokens, COLS, axis=1, tiled=True)]
    all_gather x1 -> x0, waiting for transfers between devices: 51.3 us -> none  [body(): placed = lax.all_gather(stacked, 'rows', axis=0, tiled=True)]
    all_to_all x0 -> x1, waiting for transfers between devices: none -> 45.1 us  [body(): lax.all_to_all(jnp.stack([stacked] * lax.axis_size('rows')), 'rows', 0, 0)]
    reduce_scatter x1, waiting for transfers between devices: 121 us -> 106 us  [body(): lax.psum_scatter(partial_value, 'rows', scatter_dimension=0, tiled=True)]
    mul x0 -> x1, other arithmetic: none -> 9.1 us  [body(): step_rate * placed.astype(jnp.float32)]
    ppermute x2, waiting for transfers between devices: 16.6 us -> 24 us  [partner(): lax.ppermute(x, axis, [(i, i ^ 1 << bit) for i in range(lax.axis_size(axi...]
    all_to_all x0 -> x1, starting transfers between devices: none -> 5.94 us  [body(): lax.all_to_all(jnp.stack([stacked] * lax.axis_size('rows')), 'rows', 0, 0)]
  transfers between devices with their start and end apart: 8 -> 8, of which waited for: 5 -> 6; matrix products, arithmetic and copies ran while one was open for 12% -> 10% of each run, Pallas kernels for 0% -> 0%
where the time goes in v1:
time: 579 us; the launch traced here: 578 us
  waiting for transfers between devices  467 us (81%)
  matrix products  34.2 us (6%)
  other arithmetic  29 us (5%)
  local copies, waits for them, and re-layouts  24.6 us (4%)
  between operations  14.6 us (3%)
  starting transfers between devices  8.89 us (2%)
    all_gather x1, waiting for transfers between devices, body(): lax.all_gather(tokens, COLS, axis=1, tiled=True)  146 us
    reduce_scatter x3, waiting for transfers between devices, reduced_to_own(): pieces = lax.psum_scatter(pieces, axes[k], scatter_dimension=0, tiled=True)  144 us
    reduce_scatter x1, waiting for transfers between devices, body(): lax.psum_scatter(partial_value, 'rows', scatter_dimension=0, tiled=True)  106 us
    all_to_all x1, waiting for transfers between devices, body(): lax.all_to_all(jnp.stack([stacked] * lax.axis_size('rows')), 'rows', 0, 0)  45.1 us
    ppermute x2, waiting for transfers between devices, partner(): lax.ppermute(x, axis, [(i, i ^ 1 << bit) for i in range(lax.axis_size(axi...  24 us
  transfers between devices with their start and end apart: 8, of which 6 were waited for; matrix products, arithmetic and copies ran while one was open for 10% of the time, Pallas kernels for 0%

profile of v1, /device:TPU:1, one launch (start us, length us, event | category | flops | bytes accessed | tf_op | source)
XLA Modules:
  0.0 578.2 jit_solution(624135430914134308)
XLA Ops:
  8.0 146.2 %all-gather.2.cloned.1.call-done = bf16[512,6144]{0,1:T(8,128)(2,1)} async-done(((bf16[512,192]{0,1:T(8,128)(2,1)}), bf16[512,6144]{0,1:T(8,128)(2,1)}) %all-gather.2.cloned.1.call-update) | async-done | bytes 6291472 | tf_op jit(solution)/shard_map/all_gather | solution.py:63
  154.1 9.3 %fusion.15 = f32[6144,512]{1,0:T(8,128)} fusion(bf16[512,6144]{0,1:T(8,128)(2,1)} %all-gather.2.cloned.1.call-done, bf16[512,512]{1,0:T(8,128)(2,1)S(1)} %copy-done), kind=kOutput, calls=%fused_computation.31 | convolution fusion | flops 3221225472 | bytes 19398656 | tf_op jit(solution)/shard_map/dot_general | solution.py:62
  163.5 9.4 %fusion.16 = f32[512,6144]{0,1:T(8,128)} fusion(bf16[512,512]{1,0:T(8,128)(2,1)S(1)} %copy-done, bf16[6144,512]{1,0:T(8,128)(2,1)} %param.6), kind=kOutput, calls=%fused_computation.32 | convolution fusion | flops 3221225472 | bytes 19398656 | tf_op jit(solution)/shard_map/dot_general | solution.py:68
  172.9 11.5 %copy.15 = f32[4,4,2,512,192]{3,4,2,1,0:T(8,128)} copy(f32[4,4,2,512,192]{3,4,1,2,0:T(8,128)} %bitcast.44) | data formatting | bytes 25165824 | tf_op jit(solution)/shard_map/transpose | solution.py:20
  184.5 106.4 %reduce-scatter.5.cloned.1.call-done = f32[1536,512]{1,0:T(8,128)} async-done(((f32[6144,512]{1,0:T(8,128)}), f32[1536,512]{1,0:T(8,128)}) %reduce-scatter.5.cloned.1.call-update) | async-done | bytes 3145744 | tf_op jit(solution)/shard_map/reduce_scatter | solution.py:74
  290.8 3.3 dynamic-slice_bitcast_fusion
  294.2 1.2 collective-permute-start
  295.4 111.8 %reduce-scatter.7.cloned.1.call-done = f32[8,512,192]{1,2,0:T(8,128)} async-done(((f32[32,512,192]{1,2,0:T(8,128)}), f32[8,512,192]{1,2,0:T(8,128)}) %reduce-scatter.7.cloned.1.call-update) | async-done | bytes 3145744 | tf_op jit(solution)/shard_map/reduce_scatter | solution.py:22
  407.2 6.3 %multiply_reduce_fusion = (f32[]{:T(128)}, f32[1,768,1024]{2,1,0:T(8,128)}) fusion(f32[1,768,512]{2,1,0:T(8,128)S(1)} %get-tuple-element.7, f32[1,768,512]{2,1,0:T(8,128)} %bitcast.2, pred[]{:T(512)S(6)} %eq.6, f32[1,768,1024]{2,1,0:T(8,128)} %param.7), kind=kLoop, calls=%fused_computation.11 | loop fusion | flops 5505023 | bytes 9437189 | tf_op jit(solution)/shard_map/reduce_sum | solution.py:41
  414.1 4.3 fusion.7
  418.4 5.2 add_convert_fusion.1
  423.7 1.4 convolution_convert_fusion
  425.1 4.6 fusion.2
  429.6 2.9 reshape.101
  432.5 3.2 constant_dynamic-slice_fusion.1
  436.0 1.6 collective-permute-start.1
  437.8 24.0 %collective-permute-done.1 = bf16[768,512]{1,0:T(8,128)(2,1)S(1)} collective-permute-done((bf16[768,512]{1,0:T(8,128)(2,1)S(1)}, bf16[768,512]{1,0:T(8,128)(2,1)S(1)}, u32[]{:S(2)}, u32[]{:S(2)}) %collective-permute-start.1) | collective-permute-done | bytes 786464 | tf_op jit(solution)/shard_map/ppermute | solution.py:37
  462.4 3.2 stack.2
  465.6 5.9 %all-to-all-start = ((bf16[4,1536,512]{2,1,0:T(8,128)(2,1)}), bf16[4,1536,512]{2,1,0:T(8,128)(2,1)}, u32[]{:S(2)}, u32[]{:S(2)}) async-start(bf16[4,1536,512]{2,1,0:T(8,128)(2,1)} %stack.2), calls=%async_computation.1 | async-start | bytes 12582912 | tf_op jit(solution)/shard_map/all_to_all | solution.py:96
  472.1 32.3 %reduce-scatter.11.cloned.1.call-done = f32[1,512,192]{1,2,0:T(8,128)} async-done(((f32[2,512,192]{1,2,0:T(8,128)}), f32[1,512,192]{1,2,0:T(8,128)}) %reduce-scatter.11.cloned.1.call-update) | async-done | bytes 393232 | tf_op jit(solution)/shard_map/reduce_scatter | solution.py:22
  504.4 1.7 convert_bitcast_fusion
  506.1 45.1 %all-to-all-done = bf16[4,1536,512]{2,1,0:T(8,128)(2,1)} async-done(((bf16[4,1536,512]{2,1,0:T(8,128)(2,1)}), bf16[4,1536,512]{2,1,0:T(8,128)(2,1)}, u32[]{:S(2)}, u32[]{:S(2)}) %all-to-all-start) | async-done | bytes 6291488 | tf_op jit(solution)/shard_map/all_to_all | solution.py:96
  551.2 9.1 %convert_multiply_fusion = f32[4,1536,512]{2,1,0:T(8,128)} fusion(bf16[4,1536,512]{2,1,0:T(8,128)(2,1)} %all-to-all-done), kind=kLoop, calls=%fused_computation.2 | loop fusion | flops 6291456 | bytes 18874368 | tf_op jit(solution)/shard_map/mul | solution.py:98
  560.3 11.3 %fusion = bf16[6144,512]{1,0:T(8,128)(2,1)} fusion(f32[4,1536,512]{2,1,0:T(8,128)} %convert_multiply_fusion, bf16[6144,512]{1,0:T(8,128)(2,1)} %param.6), kind=kLoop, calls=%fused_computation.1 | loop fusion | flops 9437184 | bytes 25165824 | tf_op jit(solution)/shard_map/convert_element_type | solution.py:98
  (19 shorter events, 2.5 us)
Async XLA Ops:
  7.2 147.0 %copy-start = (bf16[512,512]{1,0:T(8,128)(2,1)S(1)}, bf16[512,512]{1,0:T(8,128)(2,1)}, u32[]{:S(2)}) copy-start(bf16[512,512]{1,0:T(8,128)(2,1)} %param.5) | copy-start | bytes 1572868
  7.2 146.9 %all-gather.2.cloned.1.call-start = ((), (), s32[]{:S(2)}) async-start(), calls=%async_computation.5 | async-start | bytes 6488064 | tf_op jit(solution)/shard_map/all_gather | solution.py:63
  7.9 282.9 %reduce-scatter.5.cloned.1.call-start = ((), (), s32[]{:S(2)}) async-start(), calls=%async_computation.6 | async-start | bytes 15728640 | tf_op jit(solution)/shard_map/reduce_scatter | solution.py:74
  163.5 243.7 %reduce-scatter.7.cloned.1.call-start = ((), (), s32[]{:S(2)}) async-start(), calls=%async_computation.7 | async-start | bytes 15728640 | tf_op jit(solution)/shard_map/reduce_scatter | solution.py:22
  184.4 287.1 %reduce-scatter.9.cloned.1.call-start = ((), (), s32[]{:S(2)}) async-start(), calls=%async_computation.8 | async-start | bytes 3932160 | tf_op jit(solution)/shard_map/reduce_scatter | solution.py:22
  294.2 113.0 %collective-permute-start = (f32[768,512]{1,0:T(8,128)}, f32[768,512]{1,0:T(8,128)}, u32[]{:S(2)}, u32[]{:S(2)}) collective-permute-start(f32[768,512]{1,0:T(8,128)} %get-tuple-element.6), channel_id=1, source_target_pairs={{0,1},{1,0},{2,3},{3,2},{4,5},{5,4},{6,7},{7,6},{8,9},{9,8},{10,11... | collective-permute-start | bytes 4718600 | tf_op jit(solution)/shard_map/ppermute | solution.py:37
  436.0 25.8 %collective-permute-start.1 = (bf16[768,512]{1,0:T(8,128)(2,1)S(1)}, bf16[768,512]{1,0:T(8,128)(2,1)S(1)}, u32[]{:S(2)}, u32[]{:S(2)}) collective-permute-start(bf16[768,512]{1,0:T(8,128)(2,1)S(1)} %bitcast.48), channel_id=1, source_target_pairs={{0,1},{1,0},{2,3},{3,2},{4,5},{5,4},{6,7},{7,6},{8,9},{9,8},{10,11... | collective-permute-start | bytes 2359304 | tf_op jit(solution)/shard_map/ppermute | solution.py:37
  465.6 85.6 %all-to-all-start = ((bf16[4,1536,512]{2,1,0:T(8,128)(2,1)}), bf16[4,1536,512]{2,1,0:T(8,128)(2,1)}, u32[]{:S(2)}, u32[]{:S(2)}) async-start(bf16[4,1536,512]{2,1,0:T(8,128)(2,1)} %stack.2), calls=%async_computation.1 | async-start | bytes 12582912 | tf_op jit(solution)/shard_map/all_to_all | solution.py:96
  471.5 32.9 %reduce-scatter.11.cloned.1.call-start = ((), (), s32[]{:S(2)}) async-start(), calls=%async_computation.9 | async-start | bytes 1179648 | tf_op jit(solution)/shard_map/reduce_scatter | solution.py:22
  560.3 11.3 %copy-start.1 = (bf16[512,512]{1,0:T(8,128)(2,1)S(1)}, bf16[512,512]{1,0:T(8,128)(2,1)}, u32[]{:S(2)}) copy-start(bf16[512,512]{1,0:T(8,128)(2,1)} %param.5) | copy-start | bytes 1572868
Sparse Core Ops, SparseCore 0:
  9.6 144.4 all-gather.1
  163.6 127.2 reduce-scatter.4
  293.3 113.7 reduce-scatter.6
  409.4 42.2 reduce-scatter.8
  474.4 30.0 reduce-scatter.10
